TPU v7x, 32 devices: a whole 2x2x4 slice. The times are simulated.
32 devices in a mesh: mesh: 8 (over z, x), field: 4 (over y, core).
Axes of the slice: x: 2, y: 2, z: 4, core: 2. Of those that a mesh axis runs over, the one named last changes fastest.
Arguments:
- velocity: float32 [3, 32, 1024], P(None, ('mesh', 'field')), may hold values from -4 to 4
- pressure: float32 [32, 1024], P(('mesh', 'field')), may hold values from -128 to 128
- fields: bfloat16 [3, 256, 32, 1024], P(None, 'field', 'mesh'), may hold values from -1.8 to 1.8
- brownian: bfloat16 [3, 256, 32, 1024], P(None, 'field', 'mesh'), may hold values from -4 to 4
Outputs:
- new_fields: bfloat16 [3, 256, 32, 1024], P(None, 'field', 'mesh')
- new_velocity: float32 [3, 32, 1024], P(None, ('mesh', 'field'))
All inputs are finite; a program needn't handle non-finite values.
Results may differ from a plain program's by a relative error of at most 0.001.
Values sent between devices are 32-bit elements; how exact they have to be, the bound alone decides.
A program may use at most 64 MiB of HBM per device.

v0:
```python
import jax
import jax.numpy as jnp
from jax import lax
from jax.sharding import PartitionSpec as P

NF = 256
NY = 32
NZ = 32
SWEEPS = 4


time_step = 0.02
axial_weight = 400.0
transverse_weight = 40.0
weissenberg = 0.5
max_stretch = 50.0
polymer_viscosity = 40.0
noise_scale = (0.02 / 0.5) ** 0.5
diagonal_weight = 1.0 / 0.02 + 2.0 * 400.0 + 4.0 * 40.0
index_table = ((0, 1, 2), (1, 3, 4), (2, 4, 5))
component_pairs = ((0, 0), (0, 1), (0, 2), (1, 1), (1, 2), (2, 2))


def with_halo(block, sides, width):
    for axis, dim in sides:
        count = lax.axis_size(axis)
        forward = [(i, i + 1) for i in range(count - 1)]
        backward = [(target, source) for source, target in forward]
        low = lax.ppermute(
            lax.slice_in_dim(block, block.shape[dim] - width, None, axis=dim), axis, forward
        )
        high = lax.ppermute(lax.slice_in_dim(block, 0, width, axis=dim), axis, backward)
        block = jnp.concatenate([low, block, high], axis=dim)
    return block


def plane_shifts(values):
    extent = values.shape[-1]
    leading = [(0, 0)] * (values.ndim - 1)
    along_y = jnp.pad(values, leading + [(NZ, NZ)])
    along_z = jnp.pad(values, leading + [(1, 1)])
    column = lax.broadcasted_iota(jnp.int32, (extent,), 0) % NZ
    upper_keep = (column < NZ - 1).astype(values.dtype)
    lower_keep = (column > 0).astype(values.dtype)
    return (
        along_y[..., 2 * NZ :],
        along_y[..., :extent],
        along_z[..., 2:] * upper_keep,
        along_z[..., :extent] * lower_keep,
    )


def derivatives(padded):
    interior = padded[:, 1:-1]
    y_plus, y_minus, z_plus, z_minus = plane_shifts(interior)
    return (
        (padded[:, 2:] - padded[:, :-2]) * 0.5,
        (y_plus - y_minus) * 0.5,
        (z_plus - z_minus) * 0.5,
    )


def velocity_gradient(padded):
    stacked = jnp.stack(derivatives(padded), axis=1)
    return stacked.reshape(9, stacked.shape[2], stacked.shape[3])


def advance(fields, brownian, gradient):
    current = fields.astype(jnp.float32)
    increments = brownian.astype(jnp.float32)
    length_sq = current[0] * current[0] + current[1] * current[1] + current[2] * current[2]
    spring = 1.0 / (1.0 - length_sq / max_stretch)
    drift_terms = []
    for out_axis in range(3):
        stretch = (
            gradient[3 * out_axis][None] * current[0]
            + gradient[3 * out_axis + 1][None] * current[1]
            + gradient[3 * out_axis + 2][None] * current[2]
        )
        drift_terms.append(stretch - spring * current[out_axis] / (2.0 * weissenberg))
    advanced = current + time_step * jnp.stack(drift_terms) + noise_scale * increments
    new_sq = advanced[0] * advanced[0] + advanced[1] * advanced[1] + advanced[2] * advanced[2]
    new_spring = 1.0 / (1.0 - new_sq / max_stretch)
    partial_value = jnp.stack(
        [
            jnp.sum(new_spring * advanced[left_axis] * advanced[right_axis], axis=0)
            for left_axis, right_axis in component_pairs
        ]
    )
    return (advanced.astype(jnp.bfloat16), partial_value)


def to_stress(summed):
    identity = jnp.array([1.0, 0.0, 0.0, 1.0, 0.0, 1.0], dtype=summed.dtype)[:, None, None]
    return polymer_viscosity / weissenberg * (summed / NF - identity)


def momentum_source(velocity, padded_pressure, padded_stress):
    pressure_grad = jnp.concatenate(derivatives(padded_pressure), axis=0)
    slopes = derivatives(padded_stress)
    divergence = jnp.stack(
        [
            slopes[0][index_table[out_axis][0]]
            + slopes[1][index_table[out_axis][1]]
            + slopes[2][index_table[out_axis][2]]
            for out_axis in range(3)
        ]
    )
    return velocity / time_step - pressure_grad + divergence


def fluid_mask(offset, planes, total_planes, extent):
    position = offset + lax.broadcasted_iota(jnp.int32, (planes, extent), 0)
    across = lax.broadcasted_iota(jnp.int32, (planes, extent), 1) // NZ
    blocked = (position >= total_planes // 2) & ((across < NY // 4) | (across >= NY - NY // 4))
    return jnp.where(blocked, 0.0, 1.0).astype(jnp.float32)


def relax_step(padded, source, fluid):
    interior = padded[:, 1:-1]
    y_plus, y_minus, z_plus, z_minus = plane_shifts(interior)
    along_flow = padded[:, 2:] + padded[:, :-2]
    across_flow = y_plus + y_minus + z_plus + z_minus
    return (
        fluid
        * (source + axial_weight * along_flow + transverse_weight * across_flow)
        / diagonal_weight
    )


def body(velocity, pressure, fields, brownian):
    planes = velocity.shape[1]
    extent = velocity.shape[2]
    groups = lax.axis_size("field")
    total_planes = planes * groups * lax.axis_size("mesh")
    stacked = jnp.concatenate([velocity, pressure[None]], axis=0)
    padded = with_halo(stacked, ((("mesh", "field"), 1),), 1)
    gradient = lax.all_gather(velocity_gradient(padded[:3]), "field", axis=1, tiled=True)
    new_fields, partial_value = advance(fields, brownian, gradient)
    portion = lax.psum_scatter(partial_value, "field", scatter_dimension=1, tiled=True)
    stress = to_stress(portion)
    padded_stress = with_halo(stress, ((("mesh", "field"), 1),), 1)
    source = momentum_source(velocity, padded[3:], padded_stress)
    offset = (lax.axis_index("mesh") * groups + lax.axis_index("field")) * planes
    fluid = fluid_mask(offset, planes, total_planes, extent)

    def sweep_slab(repeat, current):
        with_rim = with_halo(current, ((("mesh", "field"), 1),), 1)
        return relax_step(with_rim, source, fluid)

    new_velocity = lax.fori_loop(0, SWEEPS, sweep_slab, velocity)
    return (new_fields, new_velocity)


def solution(mesh):
    placed = (
        P(None, ("mesh", "field"), None),
        P(("mesh", "field"), None),
        P(None, "field", "mesh", None),
        P(None, "field", "mesh", None),
    )
    return jax.shard_map(
        body,
        mesh=mesh,
        in_specs=placed,
        out_specs=(P(None, "field", "mesh", None), P(None, ("mesh", "field"), None)),
        check_vma=False,
    )
```

profile of v0, /device:TPU:7, one launch (start us, length us, event | category | flops | bytes accessed | tf_op | source)
XLA Modules:
  0.0 121.9 jit_solution(7924973539030755267)
XLA Ops:
  7.2 0.0 copy-start.5
  7.2 0.0 all-reduce.11.cloned.1.call-start
  7.2 0.7 copy.53
  7.9 0.7 pad_maximum_fusion.1
  8.6 3.7 %collective-permute-start.3 = (f32[4,1,1024]{2,1,0:T(1,128)S(1)}, f32[4,1,1024]{2,1,0:T(1,128)S(1)}, u32[]{:S(2)}, u32[]{:S(2)}) collective-permute-start(f32[4,1,1024]{2,1,0:T(1,128)S(1)} %pad_maximum_fusion.1), channel_id=1, source_target_pairs={{0,1},{1,2},{2,3},{3,4},{4,5},{5,6},{6,7},{7,8},{8,9},{9,10},{10,1... | collective-permute-start | bytes 49160 | tf_op jit(solution)/shard_map/ppermute | solution.py:29
  12.3 1.9 %collective-permute-start.2 = (f32[4,1,1024]{2,1,0:T(1,128)S(1)}, f32[4,1,1024]{2,1,0:T(1,128)S(1)}, u32[]{:S(2)}, u32[]{:S(2)}) collective-permute-start(f32[4,1,1024]{2,1,0:T(1,128)S(1)} %pad_maximum_fusion.1), channel_id=1, source_target_pairs={{1,0},{2,1},{3,2},{4,3},{5,4},{6,5},{7,6},{8,7},{9,8},{10,9},{11,1... | collective-permute-start | bytes 49160 | tf_op jit(solution)/shard_map/ppermute | solution.py:32
  14.3 0.2 multiply_bitcast_fusion.1
  14.4 0.9 subtract_multiply_fusion.3
  15.4 2.3 %convert_element_type.67 = f32[3,64,4,1024]{3,2,1,0:T(4,128)S(1)} convert(bf16[3,64,4,1024]{3,2,1,0:T(4,128)(2,1)} %param.9) | non-fusion elementwise | flops 786432 | bytes 4718592 | tf_op jit(solution)/shard_map/convert_element_type | solution.py:69
  17.8 0.7 dynamic-slice
  18.4 0.8 collective-permute-done.2
  19.3 5.9 %all_gather.3 = f32[9,4,1024]{2,0,1:T(8,128)S(1)} all-gather(f32[9,1,1024]{2,0,1:T(8,128)S(1)} %reshape.184), channel_id=1, replica_groups=mesh['mesh'=8,'field'=4] {'field'}, dimensions={1}, use_global_device_ids=true | all-gather | bytes 184320 | tf_op jit(solution)/shard_map/all_gather | solution.py:138
  25.1 0.1 fusion.30
  25.4 1.0 multiply_subtract_fusion.2
  26.4 0.0 copy-start
  26.4 0.0 copy-start.1
  26.4 1.1 multiply_subtract_fusion.1
  27.5 0.3 copy-done
  27.8 0.5 copy-done.1
  28.3 3.0 %fusion.28 = (bf16[3,64,4,1024]{3,2,1,0:T(4,128)(2,1)}, f32[3,64,4,1024]{3,2,1,0:T(4,128)S(1)}) fusion(bf16[3,64,4,1024]{3,2,1,0:T(4,128)(2,1)S(1)} %copy-done.1, f32[1,64,4,1024]{3,2,1,0:T(4,128)S(1)} %get-tuple-element.90, f32[1,64,4,1024]{3,2,1,0:T(4,128)S(1)} %get-tuple-element.89, f32[1,64,4,1024]{3,2,1,0:T(4,128)S(1)} %get-tuple-element.85, ...), kind=kLoop, calls=%fused_computation.88 | loop fusion | flops 7077888 | bytes 11010048 | tf_op jit(solution)/shard_map/convert_element_type | solution.py:90
  31.3 2.0 %fusion.11 = (f32[4,1024]{1,0:T(4,128)S(1)}, f32[4,1024]{1,0:T(4,128)S(1)}, f32[4,1024]{1,0:T(4,128)S(1)}, f32[4,1024]{1,0:T(4,128)S(1)}, f32[4,1024]{1,0:T(4,128)S(1)}, /*index=5*/f32[4,1024]{1,0:T(4,128)S(1)}) fusion(f32[3,64,4,1024]{3,2,1,0:T(4,128)S(1)} %get-tuple-element.84), kind=kLoop, calls=%fused_computation.20 | loop fusion | flops 6004736 | bytes 3244032 | tf_op jit(solution)/shard_map/reduce_sum | solution.py:86
  33.4 0.6 copy-done.3
  34.1 0.0 all-reduce.11.cloned.1.call-update
  34.1 30.4 %all-reduce.11.cloned.1.call-done = f32[6,4,1024]{2,1,0:T(4,128)} async-done(((f32[6,4,1024]{2,1,0:T(4,128)}), f32[6,4,1024]{2,1,0:T(4,128)}) %all-reduce.11.cloned.1.call-update) | async-done | bytes 98320
  64.5 1.7 %fusion.14 = f32[6,1,1024]{2,1,0:T(1,128)S(1)} fusion(f32[6,4,1024]{2,1,0:T(4,128)} %all-reduce.11.cloned.1.call-done, u32[]{:T(128)} %bitcast.15, f32[6]{0:T(128)S(1)} %copy-done.4), kind=kLoop, calls=%fused_computation.41 | loop fusion | flops 18432 | bytes 49180 | tf_op jit(solution)/shard_map/mul | solution.py:95
  66.1 5.4 %collective-permute-start.5 = (f32[6,1,1024]{2,1,0:T(1,128)S(1)}, f32[6,1,1024]{2,1,0:T(1,128)S(1)}, u32[]{:S(2)}, u32[]{:S(2)}) collective-permute-start(f32[6,1,1024]{2,1,0:T(1,128)S(1)} %fusion.14), channel_id=1, source_target_pairs={{0,1},{1,2},{2,3},{3,4},{4,5},{5,6},{6,7},{7,8},{8,9},{9,10},{10,1... | collective-permute-start | bytes 73736 | tf_op jit(solution)/shard_map/ppermute | solution.py:29
  71.5 1.9 %collective-permute-start.4 = (f32[6,1,1024]{2,1,0:T(1,128)S(1)}, f32[6,1,1024]{2,1,0:T(1,128)S(1)}, u32[]{:S(2)}, u32[]{:S(2)}) collective-permute-start(f32[6,1,1024]{2,1,0:T(1,128)S(1)} %fusion.14), channel_id=1, source_target_pairs={{1,0},{2,1},{3,2},{4,3},{5,4},{6,5},{7,6},{8,7},{9,8},{10,9},{11,1... | collective-permute-start | bytes 73736 | tf_op jit(solution)/shard_map/ppermute | solution.py:32
  73.5 0.3 subtract_multiply_fusion.1
  73.7 4.7 %collective-permute-done.4 = f32[6,1,1024]{2,1,0:T(1,128)S(1)} collective-permute-done((f32[6,1,1024]{2,1,0:T(1,128)S(1)}, f32[6,1,1024]{2,1,0:T(1,128)S(1)}, u32[]{:S(2)}, u32[]{:S(2)}) %collective-permute-start.4) | collective-permute-done | bytes 24608 | tf_op jit(solution)/shard_map/ppermute | solution.py:32
  78.6 35.9 %while.13 = (s32[]{:T(128)}, f32[3,1,1024]{2,1,0:T(1,128)S(1)}, f32[3,1,1024]{2,1,0:T(1,128)S(1)}, pred[]{:T(512)}, s32[]{:T(128)}) while((s32[]{:T(128)}, f32[3,1,1024]{2,1,0:T(1,128)S(1)}, f32[3,1,1024]{2,1,0:T(1,128)S(1)}, pred[]{:T(512)}, s32[]{:T(128)}) %tuple.58), condition=%wide.region_8.9_spmd.clone, body=%wide.region_7.8_spmd.clone.sunk | while | flops 60418 | bytes 209038 | solution.py:151
  78.6 1.9 %collective-permute-start.1 = (f32[3,1,1024]{2,1,0:T(1,128)S(1)}, f32[3,1,1024]{2,1,0:T(1,128)S(1)}, u32[]{:S(2)}, u32[]{:S(2)}) collective-permute-start(f32[3,1,1024]{2,1,0:T(1,128)S(1)} %copy.52), channel_id=1, source_target_pairs={{0,1},{1,2},{2,3},{3,4},{4,5},{5,6},{6,7},{7,8},{8,9},{9,10},{10,1... | collective-permute-start | bytes 36872 | tf_op jit(solution)/shard_map/while/body/eval_jaxpr/ppermute | solution.py:29
  80.5 2.4 %collective-permute-start = (f32[3,1,1024]{2,1,0:T(1,128)S(1)}, f32[3,1,1024]{2,1,0:T(1,128)S(1)}, u32[]{:S(2)}, u32[]{:S(2)}) collective-permute-start(f32[3,1,1024]{2,1,0:T(1,128)S(1)} %copy.52), channel_id=1, source_target_pairs={{1,0},{2,1},{3,2},{4,3},{5,4},{6,5},{7,6},{8,7},{9,8},{10,9},{11,1... | collective-permute-start | bytes 36872 | tf_op jit(solution)/shard_map/while/body/eval_jaxpr/ppermute | solution.py:32
  83.0 4.4 %collective-permute-done = f32[3,1,1024]{2,1,0:T(1,128)S(1)} collective-permute-done((f32[3,1,1024]{2,1,0:T(1,128)S(1)}, f32[3,1,1024]{2,1,0:T(1,128)S(1)}, u32[]{:S(2)}, u32[]{:S(2)}) %collective-permute-start) | collective-permute-done | bytes 12320 | tf_op jit(solution)/shard_map/while/body/eval_jaxpr/ppermute | solution.py:32
  87.3 0.2 multiply_multiply_fusion.3
  87.6 1.9 %collective-permute-start.1 = (f32[3,1,1024]{2,1,0:T(1,128)S(1)}, f32[3,1,1024]{2,1,0:T(1,128)S(1)}, u32[]{:S(2)}, u32[]{:S(2)}) collective-permute-start(f32[3,1,1024]{2,1,0:T(1,128)S(1)} %copy.52), channel_id=1, source_target_pairs={{0,1},{1,2},{2,3},{3,4},{4,5},{5,6},{6,7},{7,8},{8,9},{9,10},{10,1... | collective-permute-start | bytes 36872 | tf_op jit(solution)/shard_map/while/body/eval_jaxpr/ppermute | solution.py:29
  89.5 2.4 %collective-permute-start = (f32[3,1,1024]{2,1,0:T(1,128)S(1)}, f32[3,1,1024]{2,1,0:T(1,128)S(1)}, u32[]{:S(2)}, u32[]{:S(2)}) collective-permute-start(f32[3,1,1024]{2,1,0:T(1,128)S(1)} %copy.52), channel_id=1, source_target_pairs={{1,0},{2,1},{3,2},{4,3},{5,4},{6,5},{7,6},{8,7},{9,8},{10,9},{11,1... | collective-permute-start | bytes 36872 | tf_op jit(solution)/shard_map/while/body/eval_jaxpr/ppermute | solution.py:32
  91.9 4.4 %collective-permute-done = f32[3,1,1024]{2,1,0:T(1,128)S(1)} collective-permute-done((f32[3,1,1024]{2,1,0:T(1,128)S(1)}, f32[3,1,1024]{2,1,0:T(1,128)S(1)}, u32[]{:S(2)}, u32[]{:S(2)}) %collective-permute-start) | collective-permute-done | bytes 12320 | tf_op jit(solution)/shard_map/while/body/eval_jaxpr/ppermute | solution.py:32
  96.3 0.2 multiply_multiply_fusion.3
  96.5 1.9 %collective-permute-start.1 = (f32[3,1,1024]{2,1,0:T(1,128)S(1)}, f32[3,1,1024]{2,1,0:T(1,128)S(1)}, u32[]{:S(2)}, u32[]{:S(2)}) collective-permute-start(f32[3,1,1024]{2,1,0:T(1,128)S(1)} %copy.52), channel_id=1, source_target_pairs={{0,1},{1,2},{2,3},{3,4},{4,5},{5,6},{6,7},{7,8},{8,9},{9,10},{10,1... | collective-permute-start | bytes 36872 | tf_op jit(solution)/shard_map/while/body/eval_jaxpr/ppermute | solution.py:29
  98.5 2.4 %collective-permute-start = (f32[3,1,1024]{2,1,0:T(1,128)S(1)}, f32[3,1,1024]{2,1,0:T(1,128)S(1)}, u32[]{:S(2)}, u32[]{:S(2)}) collective-permute-start(f32[3,1,1024]{2,1,0:T(1,128)S(1)} %copy.52), channel_id=1, source_target_pairs={{1,0},{2,1},{3,2},{4,3},{5,4},{6,5},{7,6},{8,7},{9,8},{10,9},{11,1... | collective-permute-start | bytes 36872 | tf_op jit(solution)/shard_map/while/body/eval_jaxpr/ppermute | solution.py:32
  100.9 4.4 %collective-permute-done = f32[3,1,1024]{2,1,0:T(1,128)S(1)} collective-permute-done((f32[3,1,1024]{2,1,0:T(1,128)S(1)}, f32[3,1,1024]{2,1,0:T(1,128)S(1)}, u32[]{:S(2)}, u32[]{:S(2)}) %collective-permute-start) | collective-permute-done | bytes 12320 | tf_op jit(solution)/shard_map/while/body/eval_jaxpr/ppermute | solution.py:32
  105.3 0.2 multiply_multiply_fusion.3
  105.5 1.9 %collective-permute-start.1 = (f32[3,1,1024]{2,1,0:T(1,128)S(1)}, f32[3,1,1024]{2,1,0:T(1,128)S(1)}, u32[]{:S(2)}, u32[]{:S(2)}) collective-permute-start(f32[3,1,1024]{2,1,0:T(1,128)S(1)} %copy.52), channel_id=1, source_target_pairs={{0,1},{1,2},{2,3},{3,4},{4,5},{5,6},{6,7},{7,8},{8,9},{9,10},{10,1... | collective-permute-start | bytes 36872 | tf_op jit(solution)/shard_map/while/body/eval_jaxpr/ppermute | solution.py:29
  107.4 2.4 %collective-permute-start = (f32[3,1,1024]{2,1,0:T(1,128)S(1)}, f32[3,1,1024]{2,1,0:T(1,128)S(1)}, u32[]{:S(2)}, u32[]{:S(2)}) collective-permute-start(f32[3,1,1024]{2,1,0:T(1,128)S(1)} %copy.52), channel_id=1, source_target_pairs={{1,0},{2,1},{3,2},{4,3},{5,4},{6,5},{7,6},{8,7},{9,8},{10,9},{11,1... | collective-permute-start | bytes 36872 | tf_op jit(solution)/shard_map/while/body/eval_jaxpr/ppermute | solution.py:32
  109.9 4.4 %collective-permute-done = f32[3,1,1024]{2,1,0:T(1,128)S(1)} collective-permute-done((f32[3,1,1024]{2,1,0:T(1,128)S(1)}, f32[3,1,1024]{2,1,0:T(1,128)S(1)}, u32[]{:S(2)}, u32[]{:S(2)}) %collective-permute-start) | collective-permute-done | bytes 12320 | tf_op jit(solution)/shard_map/while/body/eval_jaxpr/ppermute | solution.py:32
  114.2 0.2 multiply_multiply_fusion.3
  114.4 0.0 copy-start.2
  114.5 0.6 copy-done.2
  (45 shorter events, 0.4 us)
Async XLA Ops:
  7.2 10.6 %copy-start.5 = (u32[32]{0:T(128)S(1)}, u32[32]{0:T(128)}, u32[]{:S(2)}) copy-start(u32[32]{0:T(128)} %constant.164) | copy-start | bytes 388
  7.2 57.3 %all-reduce.11.cloned.1.call-start = ((), (), s32[]{:S(2)}) async-start(), calls=%async_computation | async-start | bytes 196608
  8.6 9.8 %collective-permute-start.3 = (f32[4,1,1024]{2,1,0:T(1,128)S(1)}, f32[4,1,1024]{2,1,0:T(1,128)S(1)}, u32[]{:S(2)}, u32[]{:S(2)}) collective-permute-start(f32[4,1,1024]{2,1,0:T(1,128)S(1)} %pad_maximum_fusion.1), channel_id=1, source_target_pairs={{0,1},{1,2},{2,3},{3,4},{4,5},{5,6},{6,7},{7,8},{8,9},{9,10},{10,1... | collective-permute-start | bytes 49160 | tf_op jit(solution)/shard_map/ppermute | solution.py:29
  12.3 6.9 %collective-permute-start.2 = (f32[4,1,1024]{2,1,0:T(1,128)S(1)}, f32[4,1,1024]{2,1,0:T(1,128)S(1)}, u32[]{:S(2)}, u32[]{:S(2)}) collective-permute-start(f32[4,1,1024]{2,1,0:T(1,128)S(1)} %pad_maximum_fusion.1), channel_id=1, source_target_pairs={{1,0},{2,1},{3,2},{4,3},{5,4},{6,5},{7,6},{8,7},{9,8},{10,9},{11,1... | collective-permute-start | bytes 49160 | tf_op jit(solution)/shard_map/ppermute | solution.py:32
  26.4 1.4 %copy-start = (bf16[3,64,4,1024]{3,2,1,0:T(4,128)(2,1)S(1)}, bf16[3,64,4,1024]{3,2,1,0:T(4,128)(2,1)}, u32[]{:S(2)}) copy-start(bf16[3,64,4,1024]{3,2,1,0:T(4,128)(2,1)} %param.9) | copy-start | bytes 4718596
  26.4 1.9 %copy-start.1 = (bf16[3,64,4,1024]{3,2,1,0:T(4,128)(2,1)S(1)}, bf16[3,64,4,1024]{3,2,1,0:T(4,128)(2,1)}, u32[]{:S(2)}) copy-start(bf16[3,64,4,1024]{3,2,1,0:T(4,128)(2,1)} %param.10) | copy-start | bytes 4718596
  31.3 33.2 %copy-start.4 = (f32[6]{0:T(128)S(1)}, f32[6]{0:T(128)}, u32[]{:S(2)}) copy-start(f32[6]{0:T(128)} %constant.161) | copy-start | bytes 76
  33.4 0.6 copy-start.3
  66.1 7.6 %collective-permute-start.5 = (f32[6,1,1024]{2,1,0:T(1,128)S(1)}, f32[6,1,1024]{2,1,0:T(1,128)S(1)}, u32[]{:S(2)}, u32[]{:S(2)}) collective-permute-start(f32[6,1,1024]{2,1,0:T(1,128)S(1)} %fusion.14), channel_id=1, source_target_pairs={{0,1},{1,2},{2,3},{3,4},{4,5},{5,6},{6,7},{7,8},{8,9},{9,10},{10,1... | collective-permute-start | bytes 73736 | tf_op jit(solution)/shard_map/ppermute | solution.py:29
  71.5 6.9 %collective-permute-start.4 = (f32[6,1,1024]{2,1,0:T(1,128)S(1)}, f32[6,1,1024]{2,1,0:T(1,128)S(1)}, u32[]{:S(2)}, u32[]{:S(2)}) collective-permute-start(f32[6,1,1024]{2,1,0:T(1,128)S(1)} %fusion.14), channel_id=1, source_target_pairs={{1,0},{2,1},{3,2},{4,3},{5,4},{6,5},{7,6},{8,7},{9,8},{10,9},{11,1... | collective-permute-start | bytes 73736 | tf_op jit(solution)/shard_map/ppermute | solution.py:32
  78.6 4.4 %collective-permute-start.1 = (f32[3,1,1024]{2,1,0:T(1,128)S(1)}, f32[3,1,1024]{2,1,0:T(1,128)S(1)}, u32[]{:S(2)}, u32[]{:S(2)}) collective-permute-start(f32[3,1,1024]{2,1,0:T(1,128)S(1)} %copy.52), channel_id=1, source_target_pairs={{0,1},{1,2},{2,3},{3,4},{4,5},{5,6},{6,7},{7,8},{8,9},{9,10},{10,1... | collective-permute-start | bytes 36872 | tf_op jit(solution)/shard_map/while/body/eval_jaxpr/ppermute | solution.py:29
  80.5 6.8 %collective-permute-start = (f32[3,1,1024]{2,1,0:T(1,128)S(1)}, f32[3,1,1024]{2,1,0:T(1,128)S(1)}, u32[]{:S(2)}, u32[]{:S(2)}) collective-permute-start(f32[3,1,1024]{2,1,0:T(1,128)S(1)} %copy.52), channel_id=1, source_target_pairs={{1,0},{2,1},{3,2},{4,3},{5,4},{6,5},{7,6},{8,7},{9,8},{10,9},{11,1... | collective-permute-start | bytes 36872 | tf_op jit(solution)/shard_map/while/body/eval_jaxpr/ppermute | solution.py:32
  87.6 4.4 %collective-permute-start.1 = (f32[3,1,1024]{2,1,0:T(1,128)S(1)}, f32[3,1,1024]{2,1,0:T(1,128)S(1)}, u32[]{:S(2)}, u32[]{:S(2)}) collective-permute-start(f32[3,1,1024]{2,1,0:T(1,128)S(1)} %copy.52), channel_id=1, source_target_pairs={{0,1},{1,2},{2,3},{3,4},{4,5},{5,6},{6,7},{7,8},{8,9},{9,10},{10,1... | collective-permute-start | bytes 36872 | tf_op jit(solution)/shard_map/while/body/eval_jaxpr/ppermute | solution.py:29
  89.5 6.8 %collective-permute-start = (f32[3,1,1024]{2,1,0:T(1,128)S(1)}, f32[3,1,1024]{2,1,0:T(1,128)S(1)}, u32[]{:S(2)}, u32[]{:S(2)}) collective-permute-start(f32[3,1,1024]{2,1,0:T(1,128)S(1)} %copy.52), channel_id=1, source_target_pairs={{1,0},{2,1},{3,2},{4,3},{5,4},{6,5},{7,6},{8,7},{9,8},{10,9},{11,1... | collective-permute-start | bytes 36872 | tf_op jit(solution)/shard_map/while/body/eval_jaxpr/ppermute | solution.py:32
  96.5 4.4 %collective-permute-start.1 = (f32[3,1,1024]{2,1,0:T(1,128)S(1)}, f32[3,1,1024]{2,1,0:T(1,128)S(1)}, u32[]{:S(2)}, u32[]{:S(2)}) collective-permute-start(f32[3,1,1024]{2,1,0:T(1,128)S(1)} %copy.52), channel_id=1, source_target_pairs={{0,1},{1,2},{2,3},{3,4},{4,5},{5,6},{6,7},{7,8},{8,9},{9,10},{10,1... | collective-permute-start | bytes 36872 | tf_op jit(solution)/shard_map/while/body/eval_jaxpr/ppermute | solution.py:29
  98.5 6.8 %collective-permute-start = (f32[3,1,1024]{2,1,0:T(1,128)S(1)}, f32[3,1,1024]{2,1,0:T(1,128)S(1)}, u32[]{:S(2)}, u32[]{:S(2)}) collective-permute-start(f32[3,1,1024]{2,1,0:T(1,128)S(1)} %copy.52), channel_id=1, source_target_pairs={{1,0},{2,1},{3,2},{4,3},{5,4},{6,5},{7,6},{8,7},{9,8},{10,9},{11,1... | collective-permute-start | bytes 36872 | tf_op jit(solution)/shard_map/while/body/eval_jaxpr/ppermute | solution.py:32
  105.5 4.4 %collective-permute-start.1 = (f32[3,1,1024]{2,1,0:T(1,128)S(1)}, f32[3,1,1024]{2,1,0:T(1,128)S(1)}, u32[]{:S(2)}, u32[]{:S(2)}) collective-permute-start(f32[3,1,1024]{2,1,0:T(1,128)S(1)} %copy.52), channel_id=1, source_target_pairs={{0,1},{1,2},{2,3},{3,4},{4,5},{5,6},{6,7},{7,8},{8,9},{9,10},{10,1... | collective-permute-start | bytes 36872 | tf_op jit(solution)/shard_map/while/body/eval_jaxpr/ppermute | solution.py:29
  107.4 6.8 %collective-permute-start = (f32[3,1,1024]{2,1,0:T(1,128)S(1)}, f32[3,1,1024]{2,1,0:T(1,128)S(1)}, u32[]{:S(2)}, u32[]{:S(2)}) collective-permute-start(f32[3,1,1024]{2,1,0:T(1,128)S(1)} %copy.52), channel_id=1, source_target_pairs={{1,0},{2,1},{3,2},{4,3},{5,4},{6,5},{7,6},{8,7},{9,8},{10,9},{11,1... | collective-permute-start | bytes 36872 | tf_op jit(solution)/shard_map/while/body/eval_jaxpr/ppermute | solution.py:32
  114.4 0.6 copy-start.2
Sparse Core Ops, SparseCore 0:
  34.2 30.2 all-reduce.10
where the time goes:
time: 122 us
  waiting for transfers between devices  53.4 us (44%)
  starting transfers between devices  30.2 us (25%)
  between operations  14.4 us (12%)
  other arithmetic  14.2 us (12%)
  blocking collectives  5.85 us (5%)
  local copies, waits for them, and re-layouts  3.59 us (3%)
    unnamed x2, waiting for transfers between devices  30.4 us
    ppermute x6, waiting for transfers between devices, with_halo(): lax.ppermute(lax.slice_in_dim(block, 0, width, axis=dim), axis, backward)  23 us
    ppermute x6, starting transfers between devices, with_halo(): lax.ppermute(lax.slice_in_dim(block, block.shape[dim] - width, None, axis...  16.8 us
    ppermute x6, starting transfers between devices, with_halo(): lax.ppermute(lax.slice_in_dim(block, 0, width, axis=dim), axis, backward)  13.4 us
    all_gather x1, blocking collectives, body(): lax.all_gather(velocity_gradient(padded[:3]), 'field', axis=1, tiled=True)  5.85 us
    unnamed x28, local copies, waits for them, and re-layouts  3.45 us
    convert_element_type x1, other arithmetic, advance(): return (advanced.astype(jnp.bfloat16), partial_value)  3.04 us
  transfers between devices with their start and end apart: 13, of which 7 were waited for; matrix products, arithmetic and copies ran while one was open for 4% of the time, Pallas kernels for 0%

commit v1 on v0

v1 whole, which is shorter than its diff:
```python
import functools

import jax
import jax.numpy as jnp
from jax import lax
from jax.experimental import pallas as pl
from jax.experimental.pallas import tpu as pltpu
from jax.sharding import PartitionSpec as P

NY = 32
NZ = 32
SWEEPS = 4
LANES = 128
CHUNKS = 4

time_step = 0.02
axial_weight = 400.0
transverse_weight = 40.0
weissenberg = 0.5
max_stretch = 50.0
polymer_viscosity = 40.0
noise_scale = (0.02 / 0.5) ** 0.5
diagonal_weight = 1.0 / 0.02 + 2.0 * 400.0 + 4.0 * 40.0
index_table = ((0, 1, 2), (1, 3, 4), (2, 4, 5))
component_pairs = ((0, 0), (0, 1), (0, 2), (1, 1), (1, 2), (2, 2))
diagonal_pairs = (0, 3, 5)


def plane_shifts(x):
    rows = x.shape[0]
    lane = lax.broadcasted_iota(jnp.int32, x.shape, 1)
    row = lax.broadcasted_iota(jnp.int32, x.shape, 0)
    column = lane % NZ
    ahead = pltpu.roll(x, LANES - NZ, 1)
    ahead_next = jnp.where(row == rows - 1, 0.0, pltpu.roll(ahead, rows - 1, 0))
    y_plus = jnp.where(lane >= LANES - NZ, ahead_next, ahead)
    behind = pltpu.roll(x, NZ, 1)
    behind_next = jnp.where(row == 0, 0.0, pltpu.roll(behind, 1, 0))
    y_minus = jnp.where(lane < NZ, behind_next, behind)
    z_plus = jnp.where(column < NZ - 1, pltpu.roll(x, LANES - 1, 1), 0.0)
    z_minus = jnp.where(column > 0, pltpu.roll(x, 1, 1), 0.0)
    return y_plus, y_minus, z_plus, z_minus


def step_kernel(
    subdomains, groups,
    vel, prs, fld, brn, out_fields, out_vel,
    cur, noise, base, advanced, grads, sums, vp, parts, got, stress, vout,
    load_sem, flow_sem, vp_send, vp_recv, part_send, part_recv, st_send, st_recv, out_sem,
):
    total = subdomains * groups
    halo = SWEEPS
    width = max(halo, groups)
    rows = vel.shape[1]
    count = fld.shape[1]
    packed = fld.shape[2]
    block = min(16, packed)
    chunk = count // CHUNKS
    sub = lax.axis_index("mesh")
    own = lax.axis_index("field")
    plane = sub * groups + own
    offsets = [d for d in range(-width, width + 1) if d != 0]

    def inside(d):
        return (plane + d >= 0) & (plane + d < total)

    def device(d):
        return ((plane + d) // groups, (plane + d) % groups)

    flow_loads = [
        pltpu.make_async_copy(vel, vp.at[width, pl.ds(0, 3)], flow_sem.at[0]),
        pltpu.make_async_copy(prs, vp.at[width, 3], flow_sem.at[1]),
    ]
    for copy in flow_loads:
        copy.start()
    barrier = pltpu.get_barrier_semaphore()
    partners = jnp.int32(0)
    for d in offsets:
        @pl.when(inside(d))
        def _(d=d):
            pl.semaphore_signal(
                barrier, inc=1, device_id=device(d), device_id_type=pl.DeviceIdType.MESH
            )
        partners = partners + jnp.where(inside(d), 1, 0)
    loads = []
    for number in range(CHUNKS):
        part = pl.ds(number * chunk, chunk)
        loads.append((
            pltpu.make_async_copy(fld.at[:, part], cur.at[:, part], load_sem.at[0, number]),
            pltpu.make_async_copy(brn.at[:, part], noise.at[:, part], load_sem.at[1, number]),
        ))
        for copy in loads[-1]:
            copy.start()
    for d in offsets:
        @pl.when(jnp.logical_not(inside(d)))
        def _(d=d):
            vp[width + d] = jnp.zeros(vp.shape[1:], jnp.float32)
            stress[width + d] = jnp.zeros(stress.shape[1:], jnp.float32)
    for copy in flow_loads:
        copy.wait()
    pl.semaphore_wait(barrier, partners)

    def flow_copy(d):
        return pltpu.make_async_remote_copy(
            src_ref=vp.at[width], dst_ref=vp.at[width - d],
            send_sem=vp_send.at[width + d], recv_sem=vp_recv.at[width - d],
            device_id=device(d), device_id_type=pl.DeviceIdType.MESH,
        )

    for d in offsets:
        @pl.when(inside(d))
        def _(d=d):
            flow_copy(d).start()

    relax = time_step * max_stretch / (2.0 * weissenberg)
    for number in range(CHUNKS):
        for copy in loads[number]:
            copy.wait()

        @pl.loop(number * chunk, (number + 1) * chunk, unroll=2)
        def _(n):
            for start in range(0, packed, block):
                at = pl.ds(start, block)
                now = [cur[c, n, at].astype(jnp.float32) for c in range(3)]
                square = now[0] * now[0] + now[1] * now[1] + now[2] * now[2]
                keep = 1.0 - relax * (1.0 / (max_stretch - square))
                for c in range(3):
                    base[c, n, at] = now[c] * keep + noise_scale * noise[c, n, at].astype(jnp.float32)

    def wait_flow(slot):
        pltpu.make_async_copy(vp.at[width], vp.at[slot], vp_recv.at[slot]).wait()

    for q in range(-1, groups + 1):
        d = q - own
        @pl.when((d != 0) & inside(d))
        def _(d=d):
            wait_flow(width + d)
    for q in range(groups):
        here = width + q - own
        at = pl.ds(q, rows, stride=groups)
        for a in range(3):
            centre = vp[here, a]
            y_plus, y_minus, z_plus, z_minus = plane_shifts(centre)
            scale = 0.5 * time_step
            grads[3 * a, at] = (vp[here + 1, a] - vp[here - 1, a]) * scale
            grads[3 * a + 1, at] = (y_plus - y_minus) * scale
            grads[3 * a + 2, at] = (z_plus - z_minus) * scale

    writes = []
    for start in range(0, packed, block):
        at = pl.ds(start, block)
        g = [grads[k, at] for k in range(9)]

        def one_field(n, acc):
            now = [cur[c, n, at].astype(jnp.float32) for c in range(3)]
            new = []
            for a in range(3):
                value = base[a, n, at] + (
                    g[3 * a] * now[0] + g[3 * a + 1] * now[1] + g[3 * a + 2] * now[2]
                )
                advanced[a, n, at] = value.astype(jnp.bfloat16)
                new.append(value)
            square = new[0] * new[0] + new[1] * new[1] + new[2] * new[2]
            inverse = 1.0 / (max_stretch - square)
            pulled = [inverse * value for value in new]
            return tuple(
                total_k + pulled[left] * new[right]
                for total_k, (left, right) in zip(acc, component_pairs)
            )

        zero = jnp.zeros((block, LANES), jnp.float32)
        acc = lax.fori_loop(0, count, one_field, (zero,) * 6, unroll=2)
        for k in range(6):
            sums[k, at] = acc[k]
        writes.append(pltpu.make_async_copy(
            advanced.at[:, :, at], out_fields.at[:, :, at], out_sem.at[start // block]
        ))
        writes[-1].start()

    for q in range(groups):
        for k in range(6):
            parts[q, k] = sums[k, pl.ds(q, rows, stride=groups)]

    def part_copy(r):
        to = (own + r) % groups
        return pltpu.make_async_remote_copy(
            src_ref=parts.at[to], dst_ref=got.at[r - 1],
            send_sem=part_send.at[r - 1], recv_sem=part_recv.at[r - 1],
            device_id=(sub, to), device_id_type=pl.DeviceIdType.MESH,
        )

    for r in range(1, groups):
        part_copy(r).start()

    for d in offsets:
        q = own + d
        @pl.when(inside(d) & ((q < -1) | (q > groups)))
        def _(d=d):
            wait_flow(width + d)
    reach = halo - 1
    sources = {}
    fluid = {}
    across = (
        lax.broadcasted_iota(jnp.int32, (rows, LANES), 0) * (LANES // NZ)
        + lax.broadcasted_iota(jnp.int32, (rows, LANES), 1) // NZ
    )
    solid = jnp.where((across < NY // 4) | (across >= NY - NY // 4), 1.0, 0.0)
    for d in range(-reach, reach + 1):
        here = width + d
        y_plus, y_minus, z_plus, z_minus = plane_shifts(vp[here, 3])
        slopes = (vp[here + 1, 3] - vp[here - 1, 3], y_plus - y_minus, z_plus - z_minus)
        sources[d] = [vp[here, a] * (1.0 / time_step) - 0.5 * slopes[a] for a in range(3)]
        exists = jnp.where(inside(d), 1.0 / diagonal_weight, 0.0)
        narrow = jnp.where(plane + d >= total // 2, 1.0, 0.0)
        fluid[d] = exists * (1.0 - narrow * solid)

    for r in range(1, groups):
        part_copy(r).wait_recv()
    factor = polymer_viscosity / weissenberg
    for k in range(6):
        summed = parts[own, k]
        for r in range(1, groups):
            summed = summed + got[r - 1, k]
        value = summed * (factor * max_stretch / (count * groups))
        stress[width, k] = value - factor if k in diagonal_pairs else value

    def stress_copy(d):
        parts_of = pl.ds(0, 3 if abs(d) == halo else 6)
        return pltpu.make_async_remote_copy(
            src_ref=stress.at[width, parts_of], dst_ref=stress.at[width - d, parts_of],
            send_sem=st_send.at[width + d], recv_sem=st_recv.at[width - d],
            device_id=device(d), device_id_type=pl.DeviceIdType.MESH,
        )

    near = [d for d in offsets if abs(d) <= halo]
    for d in sorted(near, key=abs):
        @pl.when(inside(d))
        def _(d=d):
            stress_copy(d).start()
    for d in sorted(near, key=abs):
        @pl.when(inside(d))
        def _(d=d):
            stress_copy(-d).wait_recv()

    for d in range(-reach, reach + 1):
        here = width + d
        along_y = {}
        along_z = {}
        for k in range(1, 6):
            y_plus, y_minus, z_plus, z_minus = plane_shifts(stress[here, k])
            along_y[k] = y_plus - y_minus
            along_z[k] = z_plus - z_minus
        for a in range(3):
            along_x = stress[here + 1, a] - stress[here - 1, a]
            slope = along_x + along_y[index_table[a][1]] + along_z[index_table[a][2]]
            sources[d][a] = sources[d][a] + 0.5 * slope

    for a in range(3):
        v = {d: vp[width + d, a] for d in range(-halo, halo + 1)}
        for sweep in range(1, SWEEPS + 1):
            left = halo - sweep
            fresh = {}
            for d in range(-left, left + 1):
                y_plus, y_minus, z_plus, z_minus = plane_shifts(v[d])
                fresh[d] = fluid[d] * (
                    sources[d][a]
                    + axial_weight * (v[d + 1] + v[d - 1])
                    + transverse_weight * ((y_plus + y_minus) + (z_plus + z_minus))
                )
            v = fresh
        vout[a] = v[0]
    last = pltpu.make_async_copy(vout, out_vel, flow_sem.at[0])
    last.start()

    for d in offsets:
        @pl.when(inside(d))
        def _(d=d):
            flow_copy(d).wait_send()
            if abs(d) <= halo:
                stress_copy(d).wait_send()
    for r in range(1, groups):
        part_copy(r).wait_send()
    for copy in writes:
        copy.wait()
    last.wait()


def body(subdomains, groups, velocity, pressure, fields, brownian):
    extent = velocity.shape[2]
    count, depth = fields.shape[1], fields.shape[2]
    rows = extent // LANES
    packed = rows * depth
    width = max(SWEEPS, groups)

    def pack(values):
        split = values.reshape(3, count, depth, rows, LANES)
        return split.transpose(0, 1, 3, 2, 4).reshape(3, count, packed, LANES)

    dma = pltpu.SemaphoreType.DMA
    anywhere = pl.BlockSpec(memory_space=pl.ANY)
    new_fields, new_velocity = pl.pallas_call(
        functools.partial(step_kernel, subdomains, groups),
        out_shape=(
            jax.ShapeDtypeStruct((3, count, packed, LANES), jnp.bfloat16),
            jax.ShapeDtypeStruct((3, rows, LANES), jnp.float32),
        ),
        in_specs=[anywhere] * 4,
        out_specs=(anywhere, anywhere),
        scratch_shapes=[
            pltpu.VMEM((3, count, packed, LANES), jnp.bfloat16),
            pltpu.VMEM((3, count, packed, LANES), jnp.bfloat16),
            pltpu.VMEM((3, count, packed, LANES), jnp.float32),
            pltpu.VMEM((3, count, packed, LANES), jnp.bfloat16),
            pltpu.VMEM((9, packed, LANES), jnp.float32),
            pltpu.VMEM((6, packed, LANES), jnp.float32),
            pltpu.VMEM((2 * width + 1, 4, rows, LANES), jnp.float32),
            pltpu.VMEM((groups, 6, rows, LANES), jnp.float32),
            pltpu.VMEM((groups - 1, 6, rows, LANES), jnp.float32),
            pltpu.VMEM((2 * width + 1, 6, rows, LANES), jnp.float32),
            pltpu.VMEM((3, rows, LANES), jnp.float32),
            dma((2, CHUNKS)),
            dma((2,)),
            dma((2 * width + 1,)),
            dma((2 * width + 1,)),
            dma((groups - 1,)),
            dma((groups - 1,)),
            dma((2 * width + 1,)),
            dma((2 * width + 1,)),
            dma((packed // min(16, packed),)),
        ],
        compiler_params=pltpu.CompilerParams(collective_id=0, has_side_effects=True),
    )(
        velocity.reshape(3, rows, LANES),
        pressure.reshape(rows, LANES),
        pack(fields),
        pack(brownian),
    )
    unpacked = new_fields.reshape(3, count, rows, depth, LANES).transpose(0, 1, 3, 2, 4)
    return (
        unpacked.reshape(3, count, depth, extent),
        new_velocity.reshape(3, 1, extent),
    )


def solution(mesh):
    placed = (
        P(None, ("mesh", "field"), None),
        P(("mesh", "field"), None),
        P(None, "field", "mesh", None),
        P(None, "field", "mesh", None),
    )
    return jax.shard_map(
        functools.partial(body, mesh.shape["mesh"], mesh.shape["field"]),
        mesh=mesh,
        in_specs=placed,
        out_specs=(P(None, "field", "mesh", None), P(None, ("mesh", "field"), None)),
        check_vma=False,
    )
```

time: 122 us -> 23.8 us (0.20)
  the two profiles are of different devices: /device:TPU:7 before, /device:TPU:0 now
where the time goes in v1:
time: 23.8 us; the launch traced here: 23.5 us
  Pallas kernels  19 us (80%)
  local copies, waits for them, and re-layouts  3.85 us (16%)
  between operations  0.65 us (3%)
    pallas_call x1, Pallas kernels, body(): pl.pallas_call(functools.partial(step_kernel, subdomains, groups), out_sh...  19 us
    unnamed x4, local copies, waits for them, and re-layouts  3.85 us

profile of v1, /device:TPU:0, one launch (start us, length us, event | category | flops | bytes accessed | tf_op | source)
XLA Modules:
  0.0 23.5 jit_solution(7750918317152346148)
XLA Ops:
  0.6 19.0 %shard_map.59 = (bf16[3,64,32,128]{3,2,1,0:T(8,128)(2,1)}, f32[3,8,128]{2,1,0:T(8,128)}) custom-call(f32[3,8,128]{2,1,0:T(8,128)} %bitcast.21, f32[8,128]{1,0:T(8,128)} %bitcast.23, bf16[3,64,32,128]{3,2,1,0:T(8,128)(2,1)} %bitcast.18, bf16[3,64,32,128]{3,2,1,0:T(8,128)(2,1)} %bitcast.19), custom_call_target="tpu_custom_call" | custom-call | tf_op jit(solution)/shard_map/pallas_call | solution.py:301
  19.7 0.0 copy-start
  19.7 3.2 %copy.16 = bf16[3,64,4,1024]{3,2,1,0:T(4,128)(2,1)} copy(bf16[3,64,4,1024]{3,2,1,0:T(4,128)(2,1)} %bitcast.20) | data formatting | bytes 3145728
  22.9 0.0 copy-done
  22.9 0.6 %copy.17 = f32[3,1,1024]{2,1,0:T(1,128)} copy(f32[3,1,1024]{2,1,0:T(1,128)S(1)} %bitcast.22) | data formatting | bytes 24576
Async XLA Ops:
  19.7 3.3 %copy-start = (f32[3,8,128]{2,1,0:T(8,128)S(1)}, f32[3,8,128]{2,1,0:T(8,128)}, u32[]{:S(2)}) copy-start(f32[3,8,128]{2,1,0:T(8,128)} %get-tuple-element.5) | copy-start | bytes 36868

commit v2 on v1

--- a/solution.py
+++ b/solution.py
@@ -12,6 +12,7 @@
 SWEEPS = 4
 LANES = 128
 CHUNKS = 4
+VMEM_LIMIT = 24 * 1024 * 1024
 
 time_step = 0.02
 axial_weight = 400.0
@@ -44,9 +45,9 @@
 
 def step_kernel(
     subdomains, groups,
-    vel, prs, fld, brn, out_fields, out_vel,
-    cur, noise, base, advanced, grads, sums, vp, parts, got, stress, vout,
-    load_sem, flow_sem, vp_send, vp_recv, part_send, part_recv, st_send, st_recv, out_sem,
+    vel, prs, fld, brn, advanced, out_base, out_flow, out_stress,
+    cur, noise, base, grads, sums, vp, parts, got, stress,
+    load_sem, flow_sem, vp_send, vp_recv, part_send, part_recv, st_send, st_recv,
 ):
     total = subdomains * groups
     halo = SWEEPS
@@ -146,7 +147,6 @@
             grads[3 * a + 1, at] = (y_plus - y_minus) * scale
             grads[3 * a + 2, at] = (z_plus - z_minus) * scale
 
-    writes = []
     for start in range(0, packed, block):
         at = pl.ds(start, block)
         g = [grads[k, at] for k in range(9)]
@@ -172,10 +172,6 @@
         acc = lax.fori_loop(0, count, one_field, (zero,) * 6, unroll=2)
         for k in range(6):
             sums[k, at] = acc[k]
-        writes.append(pltpu.make_async_copy(
-            advanced.at[:, :, at], out_fields.at[:, :, at], out_sem.at[start // block]
-        ))
-        writes[-1].start()
 
     for q in range(groups):
         for k in range(6):
@@ -198,21 +194,14 @@
         def _(d=d):
             wait_flow(width + d)
     reach = halo - 1
-    sources = {}
-    fluid = {}
-    across = (
-        lax.broadcasted_iota(jnp.int32, (rows, LANES), 0) * (LANES // NZ)
-        + lax.broadcasted_iota(jnp.int32, (rows, LANES), 1) // NZ
-    )
-    solid = jnp.where((across < NY // 4) | (across >= NY - NY // 4), 1.0, 0.0)
+    for d in range(-halo, halo + 1):
+        out_flow[halo + d] = vp[width + d, pl.ds(0, 3)]
     for d in range(-reach, reach + 1):
         here = width + d
         y_plus, y_minus, z_plus, z_minus = plane_shifts(vp[here, 3])
         slopes = (vp[here + 1, 3] - vp[here - 1, 3], y_plus - y_minus, z_plus - z_minus)
-        sources[d] = [vp[here, a] * (1.0 / time_step) - 0.5 * slopes[a] for a in range(3)]
-        exists = jnp.where(inside(d), 1.0 / diagonal_weight, 0.0)
-        narrow = jnp.where(plane + d >= total // 2, 1.0, 0.0)
-        fluid[d] = exists * (1.0 - narrow * solid)
+        for a in range(3):
+            out_base[reach + d, a] = vp[here, a] * (1.0 / time_step) - 0.5 * slopes[a]
 
     for r in range(1, groups):
         part_copy(r).wait_recv()
@@ -242,21 +231,55 @@
         def _(d=d):
             stress_copy(-d).wait_recv()
 
+    for d in range(-halo, halo + 1):
+        out_stress[halo + d] = stress[width + d]
+
+    for d in offsets:
+        @pl.when(inside(d))
+        def _(d=d):
+            flow_copy(d).wait_send()
+            if abs(d) <= halo:
+                stress_copy(d).wait_send()
+    for r in range(1, groups):
+        part_copy(r).wait_send()
+
+
+def momentum_kernel(
+    subdomains, groups, advanced, source_base, flow, stress, out_fields, out_vel, vout, out_sem
+):
+    write = pltpu.make_async_copy(advanced, out_fields, out_sem.at[0])
+    write.start()
+    total = subdomains * groups
+    halo = SWEEPS
+    reach = halo - 1
+    rows = flow.shape[2]
+    plane = lax.axis_index("mesh") * groups + lax.axis_index("field")
+    across = (
+        lax.broadcasted_iota(jnp.int32, (rows, LANES), 0) * (LANES // NZ)
+        + lax.broadcasted_iota(jnp.int32, (rows, LANES), 1) // NZ
+    )
+    solid = jnp.where((across < NY // 4) | (across >= NY - NY // 4), 1.0, 0.0)
+    sources = {}
+    fluid = {}
     for d in range(-reach, reach + 1):
-        here = width + d
+        here = halo + d
+        exists = jnp.where((plane + d >= 0) & (plane + d < total), 1.0 / diagonal_weight, 0.0)
+        narrow = jnp.where(plane + d >= total // 2, 1.0, 0.0)
+        fluid[d] = exists * (1.0 - narrow * solid)
         along_y = {}
         along_z = {}
         for k in range(1, 6):
             y_plus, y_minus, z_plus, z_minus = plane_shifts(stress[here, k])
             along_y[k] = y_plus - y_minus
             along_z[k] = z_plus - z_minus
+        sources[d] = []
         for a in range(3):
             along_x = stress[here + 1, a] - stress[here - 1, a]
             slope = along_x + along_y[index_table[a][1]] + along_z[index_table[a][2]]
-            sources[d][a] = sources[d][a] + 0.5 * slope
+            sources[d].append(source_base[reach + d, a] + 0.5 * slope)
 
     for a in range(3):
-        v = {d: vp[width + d, a] for d in range(-halo, halo + 1)}
+        v = {d: flow[halo + d, a] for d in range(-halo, halo + 1)}
         for sweep in range(1, SWEEPS + 1):
             left = halo - sweep
             fresh = {}
@@ -269,19 +292,9 @@
                 )
             v = fresh
         vout[a] = v[0]
-    last = pltpu.make_async_copy(vout, out_vel, flow_sem.at[0])
+    last = pltpu.make_async_copy(vout, out_vel, out_sem.at[1])
     last.start()
-
-    for d in offsets:
-        @pl.when(inside(d))
-        def _(d=d):
-            flow_copy(d).wait_send()
-            if abs(d) <= halo:
-                stress_copy(d).wait_send()
-    for r in range(1, groups):
-        part_copy(r).wait_send()
-    for copy in writes:
-        copy.wait()
+    write.wait()
     last.wait()
 
 
@@ -297,27 +310,27 @@
         return split.transpose(0, 1, 3, 2, 4).reshape(3, count, packed, LANES)
 
     dma = pltpu.SemaphoreType.DMA
-    anywhere = pl.BlockSpec(memory_space=pl.ANY)
-    new_fields, new_velocity = pl.pallas_call(
+    near = pl.BlockSpec(memory_space=pltpu.VMEM)
+    between = pl.pallas_call(
         functools.partial(step_kernel, subdomains, groups),
         out_shape=(
-            jax.ShapeDtypeStruct((3, count, packed, LANES), jnp.bfloat16),
-            jax.ShapeDtypeStruct((3, rows, LANES), jnp.float32),
+            pltpu.VMEM((3, count, packed, LANES), jnp.bfloat16),
+            pltpu.VMEM((2 * SWEEPS - 1, 3, rows, LANES), jnp.float32),
+            pltpu.VMEM((2 * SWEEPS + 1, 3, rows, LANES), jnp.float32),
+            pltpu.VMEM((2 * SWEEPS + 1, 6, rows, LANES), jnp.float32),
         ),
-        in_specs=[anywhere] * 4,
-        out_specs=(anywhere, anywhere),
+        in_specs=[pl.BlockSpec(memory_space=pltpu.HBM)] * 4,
+        out_specs=(near,) * 4,
         scratch_shapes=[
             pltpu.VMEM((3, count, packed, LANES), jnp.bfloat16),
             pltpu.VMEM((3, count, packed, LANES), jnp.bfloat16),
             pltpu.VMEM((3, count, packed, LANES), jnp.float32),
-            pltpu.VMEM((3, count, packed, LANES), jnp.bfloat16),
             pltpu.VMEM((9, packed, LANES), jnp.float32),
             pltpu.VMEM((6, packed, LANES), jnp.float32),
             pltpu.VMEM((2 * width + 1, 4, rows, LANES), jnp.float32),
             pltpu.VMEM((groups, 6, rows, LANES), jnp.float32),
             pltpu.VMEM((groups - 1, 6, rows, LANES), jnp.float32),
             pltpu.VMEM((2 * width + 1, 6, rows, LANES), jnp.float32),
-            pltpu.VMEM((3, rows, LANES), jnp.float32),
             dma((2, CHUNKS)),
             dma((2,)),
             dma((2 * width + 1,)),
@@ -326,15 +339,32 @@
             dma((groups - 1,)),
             dma((2 * width + 1,)),
             dma((2 * width + 1,)),
-            dma((packed // min(16, packed),)),
         ],
-        compiler_params=pltpu.CompilerParams(collective_id=0, has_side_effects=True),
+        compiler_params=pltpu.CompilerParams(
+            collective_id=0, has_side_effects=True, vmem_limit_bytes=VMEM_LIMIT
+        ),
     )(
-        velocity.reshape(3, rows, LANES),
-        pressure.reshape(rows, LANES),
-        pack(fields),
-        pack(brownian),
-    )
+        *(
+            pltpu.with_memory_space_constraint(values, pltpu.HBM)
+            for values in (
+                velocity.reshape(3, rows, LANES),
+                pressure.reshape(rows, LANES),
+                pack(fields),
+                pack(brownian),
+            )
+        )
+    )
+    new_fields, new_velocity = pl.pallas_call(
+        functools.partial(momentum_kernel, subdomains, groups),
+        out_shape=(
+            jax.ShapeDtypeStruct((3, count, packed, LANES), jnp.bfloat16),
+            jax.ShapeDtypeStruct((3, rows, LANES), jnp.float32),
+        ),
+        in_specs=[near] * 4,
+        out_specs=(pl.BlockSpec(memory_space=pltpu.HBM),) * 2,
+        scratch_shapes=[pltpu.VMEM((3, rows, LANES), jnp.float32), dma((2,))],
+        compiler_params=pltpu.CompilerParams(vmem_limit_bytes=VMEM_LIMIT),
+    )(*between)
     unpacked = new_fields.reshape(3, count, rows, depth, LANES).transpose(0, 1, 3, 2, 4)
     return (
         unpacked.reshape(3, count, depth, extent),

time: 23.8 us -> 20.4 us (0.86)
  local copies, waits for them, and re-layouts: 3.85 us -> 0 us
  Pallas kernels: 19 us -> 19.6 us
    unnamed x4 -> x0, local copies, waits for them, and re-layouts: 3.85 us -> none
    pallas_call x0 -> x1, Pallas kernels: none -> 1.62 us  [body(): pl.pallas_call(functools.partial(momentum_kernel, subdomains, groups), ou...]
    pallas_call x1, Pallas kernels: 19 us -> 17.9 us  [body(): pl.pallas_call(functools.partial(step_kernel, subdomains, groups), out_sh...]
where the time goes in v2:
time: 20.4 us; the launch traced here: 20.2 us
  Pallas kernels  19.6 us (96%)
  between operations  0.64 us (3%)
    pallas_call x1, Pallas kernels, body(): pl.pallas_call(functools.partial(step_kernel, subdomains, groups), out_sh...  17.9 us
    pallas_call x1, Pallas kernels, body(): pl.pallas_call(functools.partial(momentum_kernel, subdomains, groups), ou...  1.62 us

profile of v2, /device:TPU:0, one launch (start us, length us, event | category | flops | bytes accessed | tf_op | source)
XLA Modules:
  0.0 20.2 jit_solution(2736266565404200075)
XLA Ops:
  0.6 17.9 %shard_map.59 = (bf16[3,64,32,128]{3,2,1,0:T(8,128)(2,1)S(1)}, f32[7,3,8,128]{3,2,1,0:T(8,128)S(1)}, f32[9,3,8,128]{3,2,1,0:T(8,128)S(1)}, f32[9,6,8,128]{3,2,1,0:T(8,128)S(1)}) custom-call(f32[3,8,128]{2,1,0:T(8,128)} %bitcast.20, f32[8,128]{1,0:T(8,128)} %bitcast.21, bf16[3,64,32,128]{3,2,1,0:T(8,128)(2,1)} %bitcast.18, bf16[3,64,32,128]{3,2,1,0:T(8,128)(2,1)} %bitcast.19), custom_call_target="tpu_custom_call" | custom-call | tf_op jit(solution)/shard_map/pallas_call | solution.py:314
  18.6 1.6 %shard_map.60 = (bf16[3,64,32,128]{3,2,1,0:T(8,128)(2,1)}, f32[3,8,128]{2,1,0:T(8,128)}) custom-call(bf16[3,64,32,128]{3,2,1,0:T(8,128)(2,1)S(1)} %get-tuple-element.8.advanced, f32[7,3,8,128]{3,2,1,0:T(8,128)S(1)} %get-tuple-element.9.source_base, f32[9,3,8,128]{3,2,1,0:T(8,128)S(1)} %get-tuple-element.10.flow, f32[9,6,8,128]{3,2,1,0:T(8,128)S(1)} %get-tuple-element.11.stress), custom_call_target="tpu_custom_call" | custom-call | tf_op jit(solution)/shard_map/pallas_call | solution.py:357

commit v3 on v2

--- a/solution.py
+++ b/solution.py
@@ -108,8 +108,16 @@
             device_id=device(d), device_id_type=pl.DeviceIdType.MESH,
         )
 
-    for d in offsets:
-        @pl.when(inside(d))
+    def urgent(d):
+        ahead = (plane + d) // groups - sub
+        return (
+            (ahead == 0)
+            | ((ahead == 1) & (own == groups - 1))
+            | ((ahead == -1) & (own == 0))
+        )
+
+    for d in sorted(offsets, key=abs):
+        @pl.when(inside(d) & urgent(d))
         def _(d=d):
             flow_copy(d).start()
 
@@ -127,6 +135,11 @@
                 keep = 1.0 - relax * (1.0 / (max_stretch - square))
                 for c in range(3):
                     base[c, n, at] = now[c] * keep + noise_scale * noise[c, n, at].astype(jnp.float32)
+
+    for d in sorted(offsets, key=abs):
+        @pl.when(inside(d) & jnp.logical_not(urgent(d)))
+        def _(d=d):
+            flow_copy(d).start()
 
     def wait_flow(slot):
         pltpu.make_async_copy(vp.at[width], vp.at[slot], vp_recv.at[slot]).wait()
@@ -146,6 +159,17 @@
             grads[3 * a, at] = (vp[here + 1, a] - vp[here - 1, a]) * scale
             grads[3 * a + 1, at] = (y_plus - y_minus) * scale
             grads[3 * a + 2, at] = (z_plus - z_minus) * scale
+
+    blocks = packed // block
+    piece = block // groups
+
+    def part_copy(number, r):
+        to = (own + r) % groups
+        return pltpu.make_async_remote_copy(
+            src_ref=parts.at[number, to], dst_ref=got.at[number, r - 1],
+            send_sem=part_send.at[number, r - 1], recv_sem=part_recv.at[number, r - 1],
+            device_id=(sub, to), device_id_type=pl.DeviceIdType.MESH,
+        )
 
     for start in range(0, packed, block):
         at = pl.ds(start, block)
@@ -173,20 +197,14 @@
         for k in range(6):
             sums[k, at] = acc[k]
 
-    for q in range(groups):
-        for k in range(6):
-            parts[q, k] = sums[k, pl.ds(q, rows, stride=groups)]
-
-    def part_copy(r):
-        to = (own + r) % groups
-        return pltpu.make_async_remote_copy(
-            src_ref=parts.at[to], dst_ref=got.at[r - 1],
-            send_sem=part_send.at[r - 1], recv_sem=part_recv.at[r - 1],
-            device_id=(sub, to), device_id_type=pl.DeviceIdType.MESH,
-        )
-
-    for r in range(1, groups):
-        part_copy(r).start()
+        number = start // block
+        for q in range(groups):
+            for k in range(6):
+                parts[number, q, pl.ds(k * piece, piece)] = sums[
+                    k, pl.ds(start + q, piece, stride=groups)
+                ]
+        for r in range(1, groups):
+            part_copy(number, r).start()
 
     for d in offsets:
         q = own + d
@@ -203,15 +221,18 @@
         for a in range(3):
             out_base[reach + d, a] = vp[here, a] * (1.0 / time_step) - 0.5 * slopes[a]
 
-    for r in range(1, groups):
-        part_copy(r).wait_recv()
     factor = polymer_viscosity / weissenberg
-    for k in range(6):
-        summed = parts[own, k]
+    for number in range(blocks):
+        summed = parts[number, own]
         for r in range(1, groups):
-            summed = summed + got[r - 1, k]
+            part_copy(number, r).wait_recv()
+            summed = summed + got[number, r - 1]
         value = summed * (factor * max_stretch / (count * groups))
-        stress[width, k] = value - factor if k in diagonal_pairs else value
+        for k in range(6):
+            of_pair = value[k * piece : (k + 1) * piece]
+            if k in diagonal_pairs:
+                of_pair = of_pair - factor
+            stress[width, k, pl.ds(number * piece, piece)] = of_pair
 
     def stress_copy(d):
         parts_of = pl.ds(0, 3 if abs(d) == halo else 6)
@@ -240,8 +261,9 @@
             flow_copy(d).wait_send()
             if abs(d) <= halo:
                 stress_copy(d).wait_send()
-    for r in range(1, groups):
-        part_copy(r).wait_send()
+    for number in range(blocks):
+        for r in range(1, groups):
+            part_copy(number, r).wait_send()
 
 
 def momentum_kernel(
@@ -303,6 +325,7 @@
     count, depth = fields.shape[1], fields.shape[2]
     rows = extent // LANES
     packed = rows * depth
+    blocks = packed // min(16, packed)
     width = max(SWEEPS, groups)
 
     def pack(values):
@@ -328,15 +351,15 @@
             pltpu.VMEM((9, packed, LANES), jnp.float32),
             pltpu.VMEM((6, packed, LANES), jnp.float32),
             pltpu.VMEM((2 * width + 1, 4, rows, LANES), jnp.float32),
-            pltpu.VMEM((groups, 6, rows, LANES), jnp.float32),
-            pltpu.VMEM((groups - 1, 6, rows, LANES), jnp.float32),
+            pltpu.VMEM((blocks, groups, 6 * rows // blocks, LANES), jnp.float32),
+            pltpu.VMEM((blocks, groups - 1, 6 * rows // blocks, LANES), jnp.float32),
             pltpu.VMEM((2 * width + 1, 6, rows, LANES), jnp.float32),
             dma((2, CHUNKS)),
             dma((2,)),
             dma((2 * width + 1,)),
             dma((2 * width + 1,)),
-            dma((groups - 1,)),
-            dma((groups - 1,)),
+            dma((blocks, groups - 1)),
+            dma((blocks, groups - 1)),
             dma((2 * width + 1,)),
             dma((2 * width + 1,)),
         ],

time: 20.4 us -> 19.9 us (0.975)
  Pallas kernels: 19.6 us -> 19.1 us
    pallas_call x1, Pallas kernels: 17.9 us -> 17.4 us  [body(): pl.pallas_call(functools.partial(step_kernel, subdomains, groups), out_sh...]
where the time goes in v3:
time: 19.9 us; the launch traced here: 19.7 us
  Pallas kernels  19.1 us (96%)
  between operations  0.64 us (3%)
    pallas_call x1, Pallas kernels, body(): pl.pallas_call(functools.partial(step_kernel, subdomains, groups), out_sh...  17.4 us
    pallas_call x1, Pallas kernels, body(): pl.pallas_call(functools.partial(momentum_kernel, subdomains, groups), ou...  1.62 us

profile of v3, /device:TPU:0, one launch (start us, length us, event | category | flops | bytes accessed | tf_op | source)
XLA Modules:
  0.0 19.7 jit_solution(7130119807650533469)
XLA Ops:
  0.6 17.4 %shard_map.59 = (bf16[3,64,32,128]{3,2,1,0:T(8,128)(2,1)S(1)}, f32[7,3,8,128]{3,2,1,0:T(8,128)S(1)}, f32[9,3,8,128]{3,2,1,0:T(8,128)S(1)}, f32[9,6,8,128]{3,2,1,0:T(8,128)S(1)}) custom-call(f32[3,8,128]{2,1,0:T(8,128)} %bitcast.20, f32[8,128]{1,0:T(8,128)} %bitcast.21, bf16[3,64,32,128]{3,2,1,0:T(8,128)(2,1)} %bitcast.18, bf16[3,64,32,128]{3,2,1,0:T(8,128)(2,1)} %bitcast.19), custom_call_target="tpu_custom_call" | custom-call | tf_op jit(solution)/shard_map/pallas_call | solution.py:337
  18.1 1.6 %shard_map.60 = (bf16[3,64,32,128]{3,2,1,0:T(8,128)(2,1)}, f32[3,8,128]{2,1,0:T(8,128)}) custom-call(bf16[3,64,32,128]{3,2,1,0:T(8,128)(2,1)S(1)} %get-tuple-element.8.advanced, f32[7,3,8,128]{3,2,1,0:T(8,128)S(1)} %get-tuple-element.9.source_base, f32[9,3,8,128]{3,2,1,0:T(8,128)S(1)} %get-tuple-element.10.flow, f32[9,6,8,128]{3,2,1,0:T(8,128)S(1)} %get-tuple-element.11.stress), custom_call_target="tpu_custom_call" | custom-call | tf_op jit(solution)/shard_map/pallas_call | solution.py:380
